TPU v7x, 32 devices: a whole 2x2x4 slice. The times are simulated.
32 devices in a mesh: section: 2 (over core), seq: 4 (over y, x), mp: 4 (over z).
Axes of the slice: x: 2, y: 2, z: 4, core: 2. Of those that a mesh axis runs over, the one named last changes fastest.
Arguments:
- token_ids: int32 [2, 1024], P(None, 'seq'), may hold values from 0 to 511
- embed_table: bfloat16 [512, 4096], P(None, 'mp'), may hold values from -40 to 40
- norm_gain: bfloat16 [2, 4096], P('section', 'mp'), may hold values from 0.099609375 to 1.8984375
- short_filters: bfloat16 [2, 3, 7, 4096], P('section', None, None, 'mp'), may hold values from -2 to 2
- medium_filters: bfloat16 [2, 128, 4096], P('section', None, 'mp'), may hold values from -0.5 to 0.5
- out_weight: bfloat16 [2, 4096, 4096], P('section', 'seq', 'mp'), may hold values from -0.09375 to 0.09375
Outputs:
- streams: bfloat16 [2, 2, 1024, 4096], P('section', None, 'seq', 'mp')
All inputs are finite; a program needn't handle non-finite values.
Results may differ from a plain program's by a relative error of at most 0.018.
Values may be sent and summed in bfloat16 or wider, within the bound.
A program may use at most 64 MiB of HBM per device.

v0:
```python
import jax
import jax.numpy as jnp
from jax import lax
from jax.sharding import PartitionSpec as P

D = 4096


def passed_along(value, axis, by):
    devices = lax.axis_size(axis)
    pairs = [(i, i + by) for i in range(devices) if 0 <= i + by < devices]
    return lax.ppermute(value, axis, pairs)


def depthwise(extended, taps):
    kernel = jnp.flip(taps, 0)[:, None, :]
    result = lax.conv_general_dilated(
        extended[None],
        kernel,
        (1,),
        "VALID",
        dimension_numbers=("NWC", "WIO", "NWC"),
        feature_group_count=taps.shape[1],
        preferred_element_type=jnp.float32,
    )
    return result[0]


def mixer_layer(stream_in, gain, shorts, medium, weight_cols):
    rows = stream_in.shape[0]
    stream = stream_in.astype(jnp.float32)
    own_squares = jnp.sum(stream * stream, axis=1, keepdims=True)
    all_squares = lax.psum(own_squares, "mp")
    normed = (
        stream * lax.rsqrt(all_squares / D + 1e-06) * gain.astype(jnp.float32)[None, :]
    ).astype(jnp.bfloat16)
    short_span = shorts.shape[1] - 1
    medium_span = medium.shape[0] - 1
    lower_rim = passed_along(normed[rows - short_span :], "seq", 1)
    extended = jnp.concatenate([lower_rim, normed], axis=0)
    features = [depthwise(extended, shorts[index]).astype(jnp.bfloat16) for index in range(3)]
    product = (features[1].astype(jnp.float32) * features[2].astype(jnp.float32)).astype(
        jnp.bfloat16
    )
    product_rim = passed_along(product[rows - medium_span :], "seq", 1)
    filtered = depthwise(jnp.concatenate([product_rim, product], axis=0), medium)
    query = features[0]
    gated = (query.astype(jnp.float32) * filtered).astype(jnp.bfloat16)
    empty = jnp.zeros((rows, weight_cols.shape[1]), jnp.float32)
    piece = jax.tree.map(lambda a: lax.all_gather(a, "mp", axis=1, tiled=True), gated)
    block_rows = lax.slice_in_dim(weight_cols, 0, piece.shape[1], axis=0)
    projected = empty + jnp.dot(piece, block_rows, preferred_element_type=jnp.float32)
    return (stream + projected).astype(jnp.bfloat16)


def local(token_ids, embed_table, norm_gain, short_filters, medium_filters, out_weight):
    section_index = lax.axis_index("section")
    weight_cols = lax.all_gather(out_weight, "seq", axis=1, tiled=True)[0]
    gain = norm_gain[0]
    shorts = short_filters[0]
    medium = medium_filters[0]
    micro_count = token_ids.shape[0]
    rows = token_ids.shape[1]
    width = embed_table.shape[1]
    vocab_ids = lax.broadcasted_iota(jnp.int32, (rows, embed_table.shape[0]), 1)
    received = jnp.zeros((rows, width), jnp.bfloat16)
    results = []
    for tick_index in range(micro_count + 1):
        chosen = token_ids[min(tick_index, micro_count - 1)]
        one_hot = (chosen[:, None] == vocab_ids).astype(jnp.bfloat16)
        embedded = jnp.dot(one_hot, embed_table, preferred_element_type=jnp.float32).astype(
            jnp.bfloat16
        )
        stream_in = jnp.where(section_index == 0, embedded, received)
        result = mixer_layer(stream_in, gain, shorts, medium, weight_cols)
        results.append(result)
        if tick_index < micro_count:
            received = passed_along(result, "section", 1)
    ordered = [
        jnp.where(section_index == 0, results[index], results[index + 1])
        for index in range(micro_count)
    ]
    return jnp.stack(ordered)[None]


def solution(mesh):
    in_specs = (
        P(None, "seq"),
        P(None, "mp"),
        P("section", "mp"),
        P("section", None, None, "mp"),
        P("section", None, "mp"),
        P("section", "seq", "mp"),
    )
    out_specs = P("section", None, "seq", "mp")
    return jax.shard_map(local, mesh=mesh, in_specs=in_specs, out_specs=out_specs, check_vma=False)
```

profile of v0, /device:TPU:5, one launch (start us, length us, event | category | flops | bytes accessed | tf_op | source)
XLA Modules:
  0.0 512.7 jit_solution(5375181700684785683)
XLA Ops:
  6.5 0.8 fusion.139
  7.3 0.7 mul.112
  8.6 9.9 %psum.21 = f32[256,1]{0,1:T(1,128)S(1)} all-reduce(f32[256,1]{0,1:T(1,128)S(1)} %bitcast.136), channel_id=1, replica_groups=mesh['section'=2,'seq'=4,'mp'=4] {'mp'}, use_global_device_ids=true, to_apply=%region_1.2 | all-reduce | flops 256 | bytes 2048 | tf_op jit(solution)/shard_map/psum | solution.py:33
  18.8 3.1 collective-permute-start
  22.7 2.6 rev.25
  26.7 0.7 fusion.23
  27.9 0.8 slice_bitcast_fusion.5
  28.7 1.9 collective-permute-start.1
  31.2 0.6 copy.28
  31.9 2.3 reshape.126
  34.2 2.8 collective-permute-done.1
  37.0 1.1 maximum_bitcast_fusion.1
  38.1 15.2 %fusion.86 = bf16[1,256,1024]{2,0,1:T(2,128)(2,1)} fusion(bf16[1,383,1024]{2,1,0:T(8,128)(2,1)S(1)} %maximum_bitcast_fusion.1, f32[1,264,1024]{2,0,1:T(1,128)S(1)} %copy-done.2, bf16[128,1,1024]{2,0,1:T(8,128)(2,1)S(1)} %bitcast.116), kind=kOutput, calls=%fused_computation.73 | convolution fusion | flops 67633152 | bytes 2619392 | tf_op jit(solution)/shard_map/conv_general_dilated | solution.py:17
  53.4 0.7 all-gather.8.cloned.1.call-update
  54.3 80.5 %all-gather.10.cloned.1.call-done = bf16[1,256,4096]{2,0,1:T(2,128)(2,1)} async-done(((bf16[1,256,1024]{2,0,1:T(2,128)(2,1)}), bf16[1,256,4096]{2,0,1:T(2,128)(2,1)}) %all-gather.10.cloned.1.call-update) | async-done | bytes 2097168 | tf_op jit(solution)/shard_map/all_gather | solution.py:50
  134.8 87.3 %all-gather.8.cloned.1.call-done = bf16[1,4096,1024]{2,1,0:T(8,128)(2,1)} async-done(((bf16[1,1024,1024]{2,1,0:T(8,128)(2,1)}), bf16[1,4096,1024]{2,1,0:T(8,128)(2,1)}) %all-gather.8.cloned.1.call-update) | async-done | bytes 8388624 | tf_op jit(solution)/shard_map/all_gather | solution.py:58
  222.1 8.6 %fusion.54 = bf16[256,1024]{1,0:T(8,128)(2,1)S(1)} fusion(bf16[1,4096,1024]{2,1,0:T(8,128)(2,1)} %all-gather.8.cloned.1.call-done, bf16[1,256,4096]{2,0,1:T(2,128)(2,1)} %all-gather.10.cloned.1.call-done, bf16[256,1024]{1,0:T(8,128)(2,1)S(1)} %get-tuple-element.15), kind=kOutput, calls=%fused_computation.62 | convolution fusion | flops 2148270080 | bytes 11534336 | tf_op jit(solution)/shard_map/dot_general | solution.py:52
  230.8 1.3 collective-permute-start.2
  232.1 2.5 collective-permute-done.2
  235.2 9.7 %psum.22 = f32[256,1]{0,1:T(1,128)S(1)} all-reduce(f32[256,1]{0,1:T(1,128)S(1)} %bitcast.135), channel_id=1, replica_groups=mesh['section'=2,'seq'=4,'mp'=4] {'mp'}, use_global_device_ids=true, to_apply=%region_3.4 | all-reduce | flops 256 | bytes 2048 | tf_op jit(solution)/shard_map/psum | solution.py:33
  245.1 2.2 collective-permute-start.3
  247.3 3.2 collective-permute-done.3
  251.8 0.7 fusion.31
  253.0 0.8 slice_bitcast_fusion.4
  253.7 1.9 collective-permute-start.4
  256.9 1.3 reshape.127
  258.3 3.8 collective-permute-done.4
  262.1 1.1 maximum_bitcast_fusion.2
  263.2 15.2 %fusion.92 = bf16[1,256,1024]{2,0,1:T(2,128)(2,1)} fusion(bf16[1,383,1024]{2,1,0:T(8,128)(2,1)S(1)} %maximum_bitcast_fusion.2, f32[1,264,1024]{2,0,1:T(1,128)S(1)} %reshape.127, bf16[128,1,1024]{2,0,1:T(8,128)(2,1)S(1)} %bitcast.117), kind=kOutput, calls=%fused_computation.75 | convolution fusion | flops 67633152 | bytes 2619392 | tf_op jit(solution)/shard_map/conv_general_dilated | solution.py:17
  278.6 81.5 %all-gather.12.cloned.1.call-done = bf16[1,256,4096]{2,0,1:T(2,128)(2,1)} async-done(((bf16[1,256,1024]{2,0,1:T(2,128)(2,1)}), bf16[1,256,4096]{2,0,1:T(2,128)(2,1)}) %all-gather.12.cloned.1.call-update) | async-done | bytes 2097168 | tf_op jit(solution)/shard_map/all_gather | solution.py:50
  360.1 8.6 %fusion.59 = bf16[256,1024]{1,0:T(8,128)(2,1)S(1)} fusion(bf16[1,4096,1024]{2,1,0:T(8,128)(2,1)} %all-gather.8.cloned.1.call-done, bf16[1,256,4096]{2,0,1:T(2,128)(2,1)} %all-gather.12.cloned.1.call-done, bf16[256,1024]{1,0:T(8,128)(2,1)S(1)} %copy-done.4), kind=kOutput, calls=%fused_computation.63 | convolution fusion | flops 2148270080 | bytes 11534336 | tf_op jit(solution)/shard_map/dot_general | solution.py:52
  368.8 1.3 collective-permute-start.5
  370.1 2.5 collective-permute-done.5
  372.8 6.8 %psum.23 = f32[256,1]{0,1:T(1,128)S(1)} all-reduce(f32[256,1]{0,1:T(1,128)S(1)} %bitcast.131), channel_id=1, replica_groups=mesh['section'=2,'seq'=4,'mp'=4] {'mp'}, use_global_device_ids=true, to_apply=%region_5.6 | all-reduce | flops 256 | bytes 2048 | tf_op jit(solution)/shard_map/psum | solution.py:33
  379.9 3.1 collective-permute-start.6
  383.0 2.3 collective-permute-done.6
  386.6 0.7 fusion.39
  387.8 0.8 slice_bitcast_fusion.3
  388.6 2.4 collective-permute-start.7
  391.6 0.6 copy.48
  392.3 1.3 reshape.128
  393.6 3.3 collective-permute-done.7
  396.9 1.1 maximum_bitcast_fusion.3
  398.0 15.2 %fusion.98 = bf16[1,256,1024]{2,0,1:T(2,128)(2,1)} fusion(bf16[1,383,1024]{2,1,0:T(8,128)(2,1)S(1)} %maximum_bitcast_fusion.3, f32[1,264,1024]{2,0,1:T(1,128)S(1)} %reshape.128, bf16[128,1,1024]{2,0,1:T(8,128)(2,1)S(1)} %bitcast.118), kind=kOutput, calls=%fused_computation.77 | convolution fusion | flops 67633152 | bytes 2619392 | tf_op jit(solution)/shard_map/conv_general_dilated | solution.py:17
  413.2 1.0 copy-done.6
  414.4 81.5 %all-gather.14.cloned.1.call-done = bf16[1,256,4096]{2,0,1:T(2,128)(2,1)} async-done(((bf16[1,256,1024]{2,0,1:T(2,128)(2,1)}), bf16[1,256,4096]{2,0,1:T(2,128)(2,1)}) %all-gather.14.cloned.1.call-update) | async-done | bytes 2097168 | tf_op jit(solution)/shard_map/all_gather | solution.py:50
  495.9 8.7 %fusion.78 = bf16[1,256,1024]{2,1,0:T(8,128)(2,1)S(1)} fusion(bf16[256,1024]{1,0:T(8,128)(2,1)S(1)} %copy-done.8, bf16[1,4096,1024]{2,1,0:T(8,128)(2,1)} %all-gather.8.cloned.1.call-done, bf16[1,256,4096]{2,0,1:T(2,128)(2,1)} %all-gather.14.cloned.1.call-done, bf16[256,1024]{1,0:T(8,128)(2,1)S(1)} %get-tuple-element.6, pred[]{:T(512)S(6)} %eq.14), kind=kOutput, calls=%fused_computation.71 | convolution fusion | flops 2148532224 | bytes 12058625 | tf_op jit(solution)/shard_map/dot_general | solution.py:52
  504.7 1.1 maximum_bitcast_fusion
  (85 shorter events, 11.6 us)
Async XLA Ops:
  6.5 1.5 copy-start
  6.5 128.3 %all-gather.10.cloned.1.call-start = ((), (), s32[]{:S(2)}) async-start(), calls=%async_computation.1 | async-start | bytes 5242880 | tf_op jit(solution)/shard_map/all_gather | solution.py:50
  8.0 13.9 %copy-start.13 = (bf16[1,3,7,1024]{3,2,1,0:T(8,128)(2,1)S(1)}, bf16[1,3,7,1024]{3,2,1,0:T(8,128)(2,1)}, u32[]{:S(2)}) copy-start(bf16[1,3,7,1024]{3,2,1,0:T(8,128)(2,1)} %param.9) | copy-start | bytes 129028
  8.0 14.6 %copy-start.9 = (bf16[1,128,1024]{2,1,0:T(8,128)(2,1)S(1)}, bf16[1,128,1024]{2,1,0:T(8,128)(2,1)}, u32[]{:S(2)}) copy-start(bf16[1,128,1024]{2,1,0:T(8,128)(2,1)} %param.10) | copy-start | bytes 786436
  18.8 6.5 %collective-permute-start = (bf16[6,1024]{1,0:T(8,128)(2,1)S(1)}, bf16[6,1024]{1,0:T(8,128)(2,1)S(1)}, u32[]{:S(2)}, u32[]{:S(2)}) collective-permute-start(bf16[6,1024]{1,0:T(8,128)(2,1)S(1)} %slice.84), channel_id=1, source_target_pairs={{0,4},{4,8},{8,12},{1,5},{5,9},{9,13},{2,6},{6,10},{10,14},{3,7},{... | collective-permute-start | bytes 36872 | tf_op jit(solution)/shard_map/ppermute | solution.py:12
  25.5 0.7 copy-start.14
  28.7 8.3 %collective-permute-start.1 = (bf16[127,1024]{1,0:T(8,128)(2,1)}, bf16[127,1024]{1,0:T(8,128)(2,1)}, u32[]{:S(2)}, u32[]{:S(2)}) collective-permute-start(bf16[127,1024]{1,0:T(8,128)(2,1)} %slice_bitcast_fusion.5), channel_id=1, source_target_pairs={{0,4},{4,8},{8,12},{1,5},{5,9},{9,13},{2,6},{6,10},{10,14},{3,7},{... | collective-permute-start | bytes 780296 | tf_op jit(solution)/shard_map/ppermute | solution.py:12
  34.2 3.9 copy-start.2
  34.2 4.0 copy-start.10
  53.3 168.8 %all-gather.8.cloned.1.call-start = ((), (), s32[]{:S(2)}) async-start(), calls=%async_computation | async-start | bytes 10485760 | tf_op jit(solution)/shard_map/all_gather | solution.py:58
  54.1 306.0 %all-gather.12.cloned.1.call-start = ((), (), s32[]{:S(2)}) async-start(), calls=%async_computation.2 | async-start | bytes 5242880 | tf_op jit(solution)/shard_map/all_gather | solution.py:50
  230.8 3.8 copy-start.5
  230.8 3.8 collective-permute-start.2
  235.2 15.3 %copy-start.3 = (bf16[256,1024]{1,0:T(8,128)(2,1)}, bf16[256,1024]{1,0:T(8,128)(2,1)S(1)}, u32[]{:S(2)}) copy-start(bf16[256,1024]{1,0:T(8,128)(2,1)S(1)} %get-tuple-element.8) | copy-start | bytes 1572868
  245.1 5.4 %collective-permute-start.3 = (bf16[6,1024]{1,0:T(8,128)(2,1)S(1)}, bf16[6,1024]{1,0:T(8,128)(2,1)S(1)}, u32[]{:S(2)}, u32[]{:S(2)}) collective-permute-start(bf16[6,1024]{1,0:T(8,128)(2,1)S(1)} %slice.89), channel_id=1, source_target_pairs={{0,4},{4,8},{8,12},{1,5},{5,9},{9,13},{2,6},{6,10},{10,14},{3,7},{... | collective-permute-start | bytes 36872 | tf_op jit(solution)/shard_map/ppermute | solution.py:12
  253.7 8.3 %collective-permute-start.4 = (bf16[127,1024]{1,0:T(8,128)(2,1)}, bf16[127,1024]{1,0:T(8,128)(2,1)}, u32[]{:S(2)}, u32[]{:S(2)}) collective-permute-start(bf16[127,1024]{1,0:T(8,128)(2,1)} %slice_bitcast_fusion.4), channel_id=1, source_target_pairs={{0,4},{4,8},{8,12},{1,5},{5,9},{9,13},{2,6},{6,10},{10,14},{3,7},{... | collective-permute-start | bytes 780296 | tf_op jit(solution)/shard_map/ppermute | solution.py:12
  258.2 4.9 copy-start.11
  263.2 97.0 %copy-start.4 = (bf16[256,1024]{1,0:T(8,128)(2,1)S(1)}, bf16[256,1024]{1,0:T(8,128)(2,1)}, u32[]{:S(2)}) copy-start(bf16[256,1024]{1,0:T(8,128)(2,1)} %copy-done.3) | copy-start | bytes 1572868
  278.4 217.6 %all-gather.14.cloned.1.call-start = ((), (), s32[]{:S(2)}) async-start(), calls=%async_computation.3 | async-start | bytes 5242880 | tf_op jit(solution)/shard_map/all_gather | solution.py:50
  368.8 11.1 %copy-start.7 = (bf16[256,1024]{1,0:T(8,128)(2,1)}, bf16[256,1024]{1,0:T(8,128)(2,1)S(1)}, u32[]{:S(2)}) copy-start(bf16[256,1024]{1,0:T(8,128)(2,1)S(1)} %fusion.59) | copy-start | bytes 1572868
  368.8 3.8 collective-permute-start.5
  379.9 5.4 %collective-permute-start.6 = (bf16[6,1024]{1,0:T(8,128)(2,1)S(1)}, bf16[6,1024]{1,0:T(8,128)(2,1)S(1)}, u32[]{:S(2)}, u32[]{:S(2)}) collective-permute-start(bf16[6,1024]{1,0:T(8,128)(2,1)S(1)} %slice.94), channel_id=1, source_target_pairs={{0,4},{4,8},{8,12},{1,5},{5,9},{9,13},{2,6},{6,10},{10,14},{3,7},{... | collective-permute-start | bytes 36872 | tf_op jit(solution)/shard_map/ppermute | solution.py:12
  388.6 8.3 %collective-permute-start.7 = (bf16[127,1024]{1,0:T(8,128)(2,1)}, bf16[127,1024]{1,0:T(8,128)(2,1)}, u32[]{:S(2)}, u32[]{:S(2)}) collective-permute-start(bf16[127,1024]{1,0:T(8,128)(2,1)} %slice_bitcast_fusion.3), channel_id=1, source_target_pairs={{0,4},{4,8},{8,12},{1,5},{5,9},{9,13},{2,6},{6,10},{10,14},{3,7},{... | collective-permute-start | bytes 780296 | tf_op jit(solution)/shard_map/ppermute | solution.py:12
  393.6 4.4 copy-start.12
  413.2 1.0 copy-start.6
  413.2 1.2 copy-start.8
  495.9 9.8 %copy-start.1 = (bf16[512,1024]{1,0:T(8,128)(2,1)S(1)}, bf16[512,1024]{1,0:T(8,128)(2,1)}, u32[]{:S(2)}) copy-start(bf16[512,1024]{1,0:T(8,128)(2,1)} %param.7) | copy-start | bytes 3145732
Sparse Core Ops, SparseCore 0:
  53.5 81.3 all-gather.9
  136.7 85.4 all-gather.7
  278.5 81.5 all-gather.11
  413.3 82.5 all-gather.13
where the time goes:
time: 521 us; the launch traced here: 513 us
  waiting for transfers between devices  352 us (68%)
  matrix products  78.3 us (15%)
  blocking collectives  26.5 us (5%)
  local copies, waits for them, and re-layouts  17.8 us (3%)
  starting transfers between devices  17.8 us (3%)
  between operations  14.1 us (3%)
  other arithmetic  6.3 us (1%)
    all_gather x3, waiting for transfers between devices, mixer_layer(): lax.all_gather(a, 'mp', axis=1, tiled=True)  243 us
    all_gather x1, waiting for transfers between devices, local(): weight_cols = lax.all_gather(out_weight, 'seq', axis=1, tiled=True)[0]  87.3 us
    conv_general_dilated x12, matrix products, depthwise(): lax.conv_general_dilated(extended[None], kernel, (1,), 'VALID', dimension...  51.2 us
    psum x3, blocking collectives, mixer_layer(): all_squares = lax.psum(own_squares, 'mp')  26.5 us
    dot_general x3, matrix products, mixer_layer(): jnp.dot(piece, block_rows, preferred_element_type=jnp.float32)  26 us
    ppermute x8, waiting for transfers between devices, passed_along(): return lax.ppermute(value, axis, pairs)  20.4 us
    ppermute x8, starting transfers between devices, passed_along(): return lax.ppermute(value, axis, pairs)  17.3 us
  transfers between devices with their start and end apart: 12, of which 11 were waited for; matrix products, arithmetic and copies ran while one was open for 2% of the time, Pallas kernels for 0%

commit v1 on v0

v1 whole, which is shorter than its diff:
```python
import functools

import jax
import jax.numpy as jnp
from jax import lax
from jax.experimental import pallas as pl
from jax.experimental.pallas import tpu as pltpu
from jax.sharding import PartitionSpec as P

MESH = pl.DeviceIdType.MESH
LANES = 128
BF = jnp.bfloat16
F32 = jnp.float32


def relay_kernel(
    sizes,
    emb_ref, gain_ref, short_ref, med_ref, w_ref,
    out_ref,
    wbuf, inbuf, x, colb, sqbuf, nsend, nrim, nf, qf, ext, psend, prim, sh, medf, gbuf, acc,
    own_sem, w_send, w_recv, go_sem, in_send, in_recv, sq_send, sq_recv,
    n_send, n_recv, p_send, p_recv, up_send, up_recv, dn_send, dn_recv,
):
    n_sec, n_seq, n_mp = sizes
    micro, rows, width = emb_ref.shape
    total_width = width * n_mp
    short_len = short_ref.shape[0] // 3
    med_len = med_ref.shape[0]
    rim = psend.shape[1]
    nrim_rows = nsend.shape[1]
    blocks = rows // rim
    depth = w_ref.shape[0]
    half = depth // 2
    levels = n_seq.bit_length() - 1
    sec, seq, mp = lax.axis_index("section"), lax.axis_index("seq"), lax.axis_index("mp")

    def remote(src, dst, send, recv, **where):
        return pltpu.make_async_remote_copy(
            src_ref=src, dst_ref=dst, send_sem=send, recv_sem=recv,
            device_id=where, device_id_type=MESH,
        )

    own = pltpu.make_async_copy(
        w_ref, wbuf.at[pl.ds(pl.multiple_of(seq * depth, depth), depth)], own_sem
    )
    own.start()
    barrier = pltpu.get_barrier_semaphore()
    greeted = 0
    for axis, count, index in (("section", n_sec, sec), ("seq", n_seq, seq), ("mp", n_mp, mp)):
        for step in range(1, count):
            pl.semaphore_signal(
                barrier, inc=1, device_id={axis: lax.rem(index + step, count)}, device_id_type=MESH
            )
            greeted += 1
    pl.semaphore_wait(barrier, greeted)
    own.wait()

    def bit_of(bit):
        return lax.rem(lax.div(seq, jnp.int32(1 << bit)), jnp.int32(2))

    orders = (list(range(levels)), list(reversed(range(levels))))

    def weight_copies(level, incoming=False):
        made = []
        for part in range(2):
            order = orders[part]
            flip = order[level]
            partner = seq + (1 - 2 * bit_of(flip)) * (1 << flip)
            for k in range(1 << level):
                shard = seq
                theirs = partner
                for i in range(level):
                    change = (((k >> i) & 1) - bit_of(order[i])) * (1 << order[i])
                    shard = shard + change
                    theirs = theirs + change
                slot = (1 << level) - 1 + k
                start = pl.multiple_of((theirs if incoming else shard) * depth + part * half, half)
                place = wbuf.at[pl.ds(start, half)]
                made.append(remote(place, place, w_send.at[part, slot], w_recv.at[part, slot], seq=partner))
        return made

    def weights_start(level):
        for out in weight_copies(level):
            out.start()

    def weights_arrive(level):
        for into in weight_copies(level, True):
            into.wait_recv()

    def weights_forward():
        for level in range(1, levels):
            weights_arrive(level - 1)
            weights_start(level)

    @pl.when(sec > 0)
    def _():
        pl.semaphore_wait(go_sem, 1)

    weights_start(0)

    @pl.when(sec > 0)
    def _():
        weights_forward()

    medf[...] = med_ref[...].astype(F32)

    @pl.when(seq == 0)
    def _():
        nf[0:nrim_rows, :] = jnp.zeros((nrim_rows, width), F32)
        ext[0:rim, :] = jnp.zeros((rim, width), F32)

    def lane(c):
        return pl.ds(pl.multiple_of(c * LANES, LANES), LANES)

    chunks = width // LANES

    def relay_copy(m):
        return remote(out_ref.at[m], inbuf.at[m], in_send.at[m], in_recv.at[m], section=sec + 1)

    def relay_in(m):
        return remote(inbuf.at[m], inbuf.at[m], in_send.at[m], in_recv.at[m], section=sec)

    def square_copy(m, step):
        return remote(
            sqbuf.at[m, mp], sqbuf.at[m, mp], sq_send.at[m, step - 1], sq_recv.at[m, step - 1],
            mp=lax.rem(mp + step, n_mp),
        )

    def square_in(m, step):
        place = sqbuf.at[m, lax.rem(mp + n_mp - step, n_mp)]
        return remote(
            place, place, sq_send.at[m, step - 1], sq_recv.at[m, step - 1],
            mp=lax.rem(mp + step, n_mp),
        )

    def normed_copy(m):
        return remote(nsend.at[m], nrim.at[m], n_send.at[m], n_recv.at[m], seq=seq + 1)

    def product_copy(m):
        return remote(psend.at[m], prim.at[m], p_send.at[m], p_recv.at[m], seq=seq + 1)

    def line_copy(m, block, step, piece, up):
        place = gbuf.at[m, block, pl.ds(piece * rim, rim)]
        send, recv = (up_send, up_recv) if up else (dn_send, dn_recv)
        return remote(
            place, place, send.at[m, step, piece], recv.at[m, step, piece],
            mp=(mp + 1) if up else (mp - 1),
        )

    def gated_send(m, block, step, piece, up):
        room = (mp < n_mp - 1) if up else (mp > 0)

        @pl.when(room)
        def _():
            line_copy(m, block, step, piece, up).start()

    row_chunk = 32

    for m in range(micro):
        @pl.when(sec > 0)
        def _():
            relay_in(m).wait_recv()

        def squares(i, _):
            part = pl.ds(pl.multiple_of(i * row_chunk, row_chunk), row_chunk)

            @pl.when(sec == 0)
            def _():
                x[part, :] = emb_ref[m, part, :].astype(F32)

            @pl.when(sec > 0)
            def _():
                x[part, :] = inbuf[m, part, :].astype(F32)

            value = x[part, :]
            summed = jnp.sum(value * value, axis=1, keepdims=True)
            colb[part, :] = jnp.broadcast_to(summed, (row_chunk, LANES))
            return 0

        lax.fori_loop(0, rows // row_chunk, squares, 0)
        sqbuf[m, mp] = colb[...].T[0:8]
        for step in range(1, n_mp):
            square_copy(m, step).start()
        for step in range(1, n_mp):
            square_in(m, step).wait_recv()
        total = sqbuf[m, 0]
        for j in range(1, n_mp):
            total = total + sqbuf[m, j]
        scale = lax.rsqrt(total / total_width + 1e-06)
        colb[...] = jnp.broadcast_to(scale[0:1], (LANES, rows)).T

        def normalise(c, _):
            value = x[:, lane(c)] * colb[...] * gain_ref[0:1, lane(c)]
            rounded = value.astype(BF)
            nf[pl.ds(nrim_rows, rows), lane(c)] = rounded.astype(F32)
            nsend[m, :, lane(c)] = rounded[rows - nrim_rows:]
            return 0

        lax.fori_loop(0, chunks, normalise, 0)

        @pl.when(seq < n_seq - 1)
        def _():
            normed_copy(m).start()

        def features(block):
            sub = rim // 2

            def body(c, _):
                for piece in range(2):
                    base = block * rim + piece * sub
                    made = [None, None, None]
                    for s in range(short_len):
                        window = nf[pl.ds(nrim_rows + base - s, sub), lane(c)]
                        for f in range(3):
                            term = short_ref[pl.ds(f * short_len + s, 1), lane(c)] * window
                            made[f] = term if made[f] is None else made[f] + term
                    made = [value.astype(BF).astype(F32) for value in made]
                    product = (made[1] * made[2]).astype(BF)
                    qf[pl.ds(base, sub), lane(c)] = made[0]
                    ext[pl.ds(rim + base, sub), lane(c)] = product.astype(F32)
                    if block == blocks - 1:
                        psend[m, pl.ds(piece * sub, sub), lane(c)] = product
                return 0

            lax.fori_loop(0, chunks, body, 0)

        for block in reversed(range(blocks)):
            if block == 0:
                @pl.when(seq > 0)
                def _():
                    normed_copy(m).wait_recv()
                    nf[0:nrim_rows, :] = nrim[m].astype(F32)

            features(block)
            if block == blocks - 1:
                @pl.when(seq < n_seq - 1)
                def _():
                    product_copy(m).start()

        if m == 0:
            @pl.when(sec == 0)
            def _():
                weights_forward()

        def filtering(block):
            taps_rows = 2 * rim

            def body(c, _):
                lo = block * rim
                for b in range(8):
                    sh[b, 8:taps_rows, :] = ext[pl.ds(lo + 8 - b, taps_rows - 8), lane(c)]
                value = jnp.zeros((rim, LANES), F32)
                for b in range(8):
                    for a in range(rim // 8):
                        s = 8 * a + b
                        if s < med_len:
                            tap = medf[pl.ds(s, 1), lane(c)]
                            value = value + tap * sh[b, rim - 8 * a:2 * rim - 8 * a, :]
                here = pl.ds(lo, rim)
                gbuf[m, mp, here, lane(c)] = (qf[here, lane(c)] * value).astype(BF)
                return 0

            lax.fori_loop(0, chunks, body, 0)

        for block in reversed(range(blocks)):
            if block == 0:
                @pl.when(seq > 0)
                def _():
                    product_copy(m).wait_recv()
                    ext[0:rim, :] = prim[m].astype(F32)

            filtering(block)
            for up in (True, False):
                gated_send(m, mp, 0, block, up)

        if m == 0:
            weights_arrive(levels - 1)

            @pl.when(sec < n_sec - 1)
            def _():
                pl.semaphore_signal(go_sem, inc=1, device_id={"section": sec + 1}, device_id_type=MESH)

        cols = 256

        def add_block(block, first):
            source = pl.ds(pl.multiple_of(block * width, width), width)

            def body(c, _):
                part = pl.ds(pl.multiple_of(c * cols, cols), cols)
                value = jnp.dot(gbuf[m, block], wbuf[source, part], preferred_element_type=F32)
                if first:
                    acc[:, part] = value
                else:
                    acc[:, part] += value
                return 0

            lax.fori_loop(0, width // cols, body, 0)

        add_block(mp, True)
        for step in range(1, n_mp):
            for up in (True, False):
                here = (mp - step) if up else (mp + step)
                exists = (here >= 0) if up else (here < n_mp)

                @pl.when(exists)
                def _():
                    for piece in reversed(range(blocks)):
                        line_copy(m, here, step - 1, piece, up).wait_recv()
                        if step < n_mp - 1:
                            gated_send(m, here, step, piece, up)
                    add_block(here, False)

        def finish(i, _):
            part = pl.ds(pl.multiple_of(i * row_chunk, row_chunk), row_chunk)
            out_ref[m, part, :] = (x[part, :] + acc[part, :]).astype(BF)
            return 0

        lax.fori_loop(0, rows // row_chunk, finish, 0)

        @pl.when(sec < n_sec - 1)
        def _():
            relay_copy(m).start()

    for level in range(levels):
        for out in weight_copies(level):
            out.wait_send()
    for m in range(micro):
        @pl.when(sec < n_sec - 1)
        def _():
            relay_copy(m).wait_send()

        for step in range(1, n_mp):
            square_copy(m, step).wait_send()

        @pl.when(seq < n_seq - 1)
        def _():
            normed_copy(m).wait_send()
            product_copy(m).wait_send()

        for up in (True, False):
            room = (mp < n_mp - 1) if up else (mp > 0)
            for step in range(n_mp - 1):
                block = (mp - step) if up else (mp + step)
                exists = (block >= 0) if up else (block < n_mp)

                @pl.when(jnp.logical_and(room, exists))
                def _():
                    for piece in range(blocks):
                        line_copy(m, block, step, piece, up).wait_send()


def up16(count):
    return (count + 15) // 16 * 16


def local(sizes, token_ids, embed_table, norm_gain, short_filters, medium_filters, out_weight):
    n_sec, n_seq, n_mp = sizes
    micro, rows = token_ids.shape
    vocab, width = embed_table.shape
    ids = token_ids.reshape(micro * rows)
    one_hot = (ids[:, None] == lax.broadcasted_iota(jnp.int32, (micro * rows, vocab), 1)).astype(BF)
    embedded = jnp.dot(one_hot, embed_table, preferred_element_type=F32).astype(BF)
    embedded = embedded.reshape(micro, rows, width)
    shorts = short_filters[0].astype(F32).reshape(-1, width)
    nrim_rows = up16(short_filters.shape[2] - 1)
    rim = up16(medium_filters.shape[1])
    blocks = rows // rim
    vmem = pl.BlockSpec(memory_space=pltpu.VMEM)
    dma = pltpu.SemaphoreType.DMA
    result = pl.pallas_call(
        functools.partial(relay_kernel, sizes),
        out_shape=jax.ShapeDtypeStruct((micro, rows, width), BF),
        in_specs=[vmem, vmem, vmem, vmem, pl.BlockSpec(memory_space=pl.ANY)],
        out_specs=vmem,
        scratch_shapes=[
            pltpu.VMEM((width * n_mp, width), BF),
            pltpu.VMEM((micro, rows, width), BF),
            pltpu.VMEM((rows, width), F32),
            pltpu.VMEM((rows, LANES), F32),
            pltpu.VMEM((micro, n_mp, 8, rows), F32),
            pltpu.VMEM((micro, nrim_rows, width), BF),
            pltpu.VMEM((micro, nrim_rows, width), BF),
            pltpu.VMEM((nrim_rows + rows, width), F32),
            pltpu.VMEM((rows, width), F32),
            pltpu.VMEM((rim + rows, width), F32),
            pltpu.VMEM((micro, rim, width), BF),
            pltpu.VMEM((micro, rim, width), BF),
            pltpu.VMEM((8, 2 * rim, LANES), F32),
            pltpu.VMEM(medium_filters.shape[1:], F32),
            pltpu.VMEM((micro, n_mp, rows, width), BF),
            pltpu.VMEM((rows, width), F32),
            dma, dma((2, n_seq)), dma((2, n_seq)), pltpu.SemaphoreType.REGULAR,
            dma((micro,)), dma((micro,)), dma((micro, n_mp)), dma((micro, n_mp)),
            dma((micro,)), dma((micro,)), dma((micro,)), dma((micro,)),
            dma((micro, n_mp, blocks)), dma((micro, n_mp, blocks)),
            dma((micro, n_mp, blocks)), dma((micro, n_mp, blocks)),
        ],
        compiler_params=pltpu.CompilerParams(
            collective_id=0, has_side_effects=True, vmem_limit_bytes=56 * 1024 * 1024
        ),
    )(embedded, norm_gain.astype(F32), shorts, medium_filters[0], out_weight[0])
    return result[None]


def solution(mesh):
    sizes = tuple(mesh.shape[name] for name in ("section", "seq", "mp"))
    in_specs = (
        P(None, "seq"),
        P(None, "mp"),
        P("section", "mp"),
        P("section", None, None, "mp"),
        P("section", None, "mp"),
        P("section", "seq", "mp"),
    )
    out_specs = P("section", None, "seq", "mp")
    return jax.shard_map(
        functools.partial(local, sizes), mesh=mesh, in_specs=in_specs, out_specs=out_specs, check_vma=False
    )
```

time: 521 us -> 166 us (0.32); the launches traced: 513 us -> 166 us
  waiting for transfers between devices: 352 us -> 0 us
  Pallas kernels: 0 us -> 159 us
  matrix products: 78.3 us -> 1.73 us
  blocking collectives: 26.5 us -> 0 us
  starting transfers between devices: 17.8 us -> 0 us
  between operations: 14.1 us -> 0.01 us
  local copies, waits for them, and re-layouts: 17.8 us -> 4.49 us
    all_gather x4 -> x0, waiting for transfers between devices: 331 us -> none  [the longest x3 243 us: mixer_layer(): lax.all_gather(a, 'mp', axis=1, tiled=True)]
    pallas_call x0 -> x1, Pallas kernels: none -> 159 us  [local(): pl.pallas_call(functools.partial(relay_kernel, sizes), out_shape=jax.Shap...]
    conv_general_dilated x12 -> x0, matrix products: 51.2 us -> none  [depthwise(): lax.conv_general_dilated(extended[None], kernel, (1,), 'VALID', dimension...]
    psum x3 -> x0, blocking collectives: 26.5 us -> none  [mixer_layer(): all_squares = lax.psum(own_squares, 'mp')]
    dot_general x5 -> x1, matrix products: 27.1 us -> 1.73 us  [local(): jnp.dot(one_hot, embed_table, preferred_element_type=F32).astype(BF)]
    ppermute x8 -> x0, waiting for transfers between devices: 20.4 us -> none  [passed_along(): return lax.ppermute(value, axis, pairs)]
    ppermute x8 -> x0, starting transfers between devices: 17.3 us -> none  [passed_along(): return lax.ppermute(value, axis, pairs)]
    convert_element_type x15 -> x1, local copies, waits for them, and re-layouts: 8.37 us -> 1.45 us  [local(): shorts = short_filters[0].astype(F32).reshape(-1, width)]
  transfers between devices with their start and end apart: 12 -> 0, of which waited for: 11 -> 0; matrix products, arithmetic and copies ran while one was open for 2% -> 0% of each run, Pallas kernels for 0% -> 0%
where the time goes in v1:
time: 166 us
  Pallas kernels  159 us (96%)
  local copies, waits for them, and re-layouts  4.49 us (3%)
  matrix products  1.73 us (1%)
    pallas_call x1, Pallas kernels, local(): pl.pallas_call(functools.partial(relay_kernel, sizes), out_shape=jax.Shap...  159 us

profile of v1, /device:TPU:5, one launch (start us, length us, event | category | flops | bytes accessed | tf_op | source)
XLA Modules:
  0.0 166.1 jit_solution(561197047776221184)
XLA Ops:
  0.0 0.0 copy-start
  0.0 0.8 copy.7
  0.8 1.3 convert_element_type.15.gain_ref
  2.1 1.4 reshape.9.short_ref
  3.5 0.0 copy-done
  3.5 1.7 %convolution_convert_fusion = bf16[512,1024]{1,0:T(8,128)(2,1)} fusion(bf16[512,1024]{1,0:T(8,128)(2,1)S(1)} %copy-done, s32[512]{0:T(512)S(1)} %bitcast.12), kind=kOutput, calls=%fused_computation | convolution fusion | flops 537657344 | bytes 2099200 | tf_op jit(solution)/shard_map/dot_general | solution.py:362
  5.2 158.5 %shard_map.64 = bf16[2,256,1024]{2,1,0:T(8,128)(2,1)} custom-call(bf16[2,256,1024]{2,1,0:T(8,128)(2,1)} %bitcast.9, f32[1,1024]{1,0:T(1,128)} %convert_element_type.15.gain_ref, f32[21,1024]{1,0:T(8,128)} %reshape.9.short_ref, bf16[128,1024]{1,0:T(8,128)(2,1)} %bitcast.10, bf16[1024,1024]{1,0:T(8,128)(2,1)} %bitcast.8), custom_call_target="tpu_custom_call" | custom-call | tf_op jit(solution)/shard_map/pallas_call | solution.py:370
  163.8 2.3 %copy.9 = bf16[1,2,256,1024]{3,2,1,0:T(8,128)(2,1)} copy(bf16[1,2,256,1024]{3,2,1,0:T(8,128)(2,1)} %bitcast.7) | data formatting | bytes 2097152
Async XLA Ops:
  0.0 3.5 %copy-start = (bf16[512,1024]{1,0:T(8,128)(2,1)S(1)}, bf16[512,1024]{1,0:T(8,128)(2,1)}, u32[]{:S(2)}) copy-start(bf16[512,1024]{1,0:T(8,128)(2,1)} %param.7) | copy-start | bytes 3145732

commit v2 on v1

--- a/solution.py
+++ b/solution.py
@@ -17,19 +17,19 @@
     sizes,
     emb_ref, gain_ref, short_ref, med_ref, w_ref,
     out_ref,
-    wbuf, inbuf, x, colb, sqbuf, nsend, nrim, nf, qf, ext, psend, prim, sh, medf, gbuf, acc,
+    wbuf, inbuf, x, gainf, shortf, colb, sqbuf, nsend, nrim, nf, qf, ext, psend, prim, sh, medf, gbuf, acc,
     own_sem, w_send, w_recv, go_sem, in_send, in_recv, sq_send, sq_recv,
     n_send, n_recv, p_send, p_recv, up_send, up_recv, dn_send, dn_recv,
 ):
     n_sec, n_seq, n_mp = sizes
     micro, rows, width = emb_ref.shape
     total_width = width * n_mp
-    short_len = short_ref.shape[0] // 3
-    med_len = med_ref.shape[0]
+    short_len = short_ref.shape[2]
+    med_len = med_ref.shape[1]
     rim = psend.shape[1]
     nrim_rows = nsend.shape[1]
     blocks = rows // rim
-    depth = w_ref.shape[0]
+    depth = w_ref.shape[1]
     half = depth // 2
     levels = n_seq.bit_length() - 1
     sec, seq, mp = lax.axis_index("section"), lax.axis_index("seq"), lax.axis_index("mp")
@@ -41,7 +41,7 @@
         )
 
     own = pltpu.make_async_copy(
-        w_ref, wbuf.at[pl.ds(pl.multiple_of(seq * depth, depth), depth)], own_sem
+        w_ref.at[0], wbuf.at[pl.ds(pl.multiple_of(seq * depth, depth), depth)], own_sem
     )
     own.start()
     barrier = pltpu.get_barrier_semaphore()
@@ -102,7 +102,9 @@
     def _():
         weights_forward()
 
-    medf[...] = med_ref[...].astype(F32)
+    medf[...] = med_ref[0].astype(F32)
+    shortf[...] = short_ref[0].astype(F32)
+    gainf[...] = gain_ref[...].astype(F32)
 
     @pl.when(seq == 0)
     def _():
@@ -156,7 +158,25 @@
 
     row_chunk = 32
 
-    for m in range(micro):
+    def forward(m, step):
+        for up in (True, False):
+            here = (mp - step) if up else (mp + step)
+            exists = (here >= 0) if up else (here < n_mp)
+
+            @pl.when(exists)
+            def _():
+                for piece in reversed(range(blocks)):
+                    line_copy(m, here, step - 1, piece, up).wait_recv()
+                    if step < n_mp - 1:
+                        gated_send(m, here, step, piece, up)
+
+    def front(m):
+        pending = list(range(1, n_mp - 1)) if m > 0 else []
+
+        def forward_one():
+            if pending:
+                forward(m - 1, pending.pop(0))
+
         @pl.when(sec > 0)
         def _():
             relay_in(m).wait_recv()
@@ -166,13 +186,13 @@
 
             @pl.when(sec == 0)
             def _():
-                x[part, :] = emb_ref[m, part, :].astype(F32)
+                x[m, part, :] = emb_ref[m, part, :].astype(F32)
 
             @pl.when(sec > 0)
             def _():
-                x[part, :] = inbuf[m, part, :].astype(F32)
-
-            value = x[part, :]
+                x[m, part, :] = inbuf[m, part, :].astype(F32)
+
+            value = x[m, part, :]
             summed = jnp.sum(value * value, axis=1, keepdims=True)
             colb[part, :] = jnp.broadcast_to(summed, (row_chunk, LANES))
             return 0
@@ -190,7 +210,7 @@
         colb[...] = jnp.broadcast_to(scale[0:1], (LANES, rows)).T
 
         def normalise(c, _):
-            value = x[:, lane(c)] * colb[...] * gain_ref[0:1, lane(c)]
+            value = x[m, :, lane(c)] * colb[...] * gainf[0:1, lane(c)]
             rounded = value.astype(BF)
             nf[pl.ds(nrim_rows, rows), lane(c)] = rounded.astype(F32)
             nsend[m, :, lane(c)] = rounded[rows - nrim_rows:]
@@ -201,6 +221,8 @@
         @pl.when(seq < n_seq - 1)
         def _():
             normed_copy(m).start()
+
+        forward_one()
 
         def features(block):
             sub = rim // 2
@@ -212,7 +234,7 @@
                     for s in range(short_len):
                         window = nf[pl.ds(nrim_rows + base - s, sub), lane(c)]
                         for f in range(3):
-                            term = short_ref[pl.ds(f * short_len + s, 1), lane(c)] * window
+                            term = shortf[f, pl.ds(s, 1), lane(c)] * window
                             made[f] = term if made[f] is None else made[f] + term
                     made = [value.astype(BF).astype(F32) for value in made]
                     product = (made[1] * made[2]).astype(BF)
@@ -237,6 +259,7 @@
                 def _():
                     product_copy(m).start()
 
+        forward_one()
         if m == 0:
             @pl.when(sec == 0)
             def _():
@@ -273,6 +296,26 @@
             for up in (True, False):
                 gated_send(m, mp, 0, block, up)
 
+        while pending:
+            forward_one()
+
+    cols = 256
+
+    def add_block(m, block, first):
+        source = pl.ds(pl.multiple_of(block * width, width), width)
+
+        def body(c, _):
+            part = pl.ds(pl.multiple_of(c * cols, cols), cols)
+            value = jnp.dot(gbuf[m, block], wbuf[source, part], preferred_element_type=F32)
+            if first:
+                acc[:, part] = value
+            else:
+                acc[:, part] += value
+            return 0
+
+        lax.fori_loop(0, width // cols, body, 0)
+
+    def back(m):
         if m == 0:
             weights_arrive(levels - 1)
 
@@ -280,39 +323,21 @@
             def _():
                 pl.semaphore_signal(go_sem, inc=1, device_id={"section": sec + 1}, device_id_type=MESH)
 
-        cols = 256
-
-        def add_block(block, first):
-            source = pl.ds(pl.multiple_of(block * width, width), width)
-
-            def body(c, _):
-                part = pl.ds(pl.multiple_of(c * cols, cols), cols)
-                value = jnp.dot(gbuf[m, block], wbuf[source, part], preferred_element_type=F32)
-                if first:
-                    acc[:, part] = value
-                else:
-                    acc[:, part] += value
-                return 0
-
-            lax.fori_loop(0, width // cols, body, 0)
-
-        add_block(mp, True)
+        add_block(m, mp, True)
         for step in range(1, n_mp):
+            if m == micro - 1 or step == n_mp - 1:
+                forward(m, step)
             for up in (True, False):
                 here = (mp - step) if up else (mp + step)
                 exists = (here >= 0) if up else (here < n_mp)
 
                 @pl.when(exists)
                 def _():
-                    for piece in reversed(range(blocks)):
-                        line_copy(m, here, step - 1, piece, up).wait_recv()
-                        if step < n_mp - 1:
-                            gated_send(m, here, step, piece, up)
-                    add_block(here, False)
+                    add_block(m, here, False)
 
         def finish(i, _):
             part = pl.ds(pl.multiple_of(i * row_chunk, row_chunk), row_chunk)
-            out_ref[m, part, :] = (x[part, :] + acc[part, :]).astype(BF)
+            out_ref[m, part, :] = (x[m, part, :] + acc[part, :]).astype(BF)
             return 0
 
         lax.fori_loop(0, rows // row_chunk, finish, 0)
@@ -320,6 +345,12 @@
         @pl.when(sec < n_sec - 1)
         def _():
             relay_copy(m).start()
+
+    for m in range(micro + 1):
+        if m < micro:
+            front(m)
+        if m > 0:
+            back(m - 1)
 
     for level in range(levels):
         for out in weight_copies(level):
@@ -361,7 +392,6 @@
     one_hot = (ids[:, None] == lax.broadcasted_iota(jnp.int32, (micro * rows, vocab), 1)).astype(BF)
     embedded = jnp.dot(one_hot, embed_table, preferred_element_type=F32).astype(BF)
     embedded = embedded.reshape(micro, rows, width)
-    shorts = short_filters[0].astype(F32).reshape(-1, width)
     nrim_rows = up16(short_filters.shape[2] - 1)
     rim = up16(medium_filters.shape[1])
     blocks = rows // rim
@@ -375,7 +405,9 @@
         scratch_shapes=[
             pltpu.VMEM((width * n_mp, width), BF),
             pltpu.VMEM((micro, rows, width), BF),
-            pltpu.VMEM((rows, width), F32),
+            pltpu.VMEM((micro, rows, width), F32),
+            pltpu.VMEM(norm_gain.shape, F32),
+            pltpu.VMEM(short_filters.shape[1:], F32),
             pltpu.VMEM((rows, LANES), F32),
             pltpu.VMEM((micro, n_mp, 8, rows), F32),
             pltpu.VMEM((micro, nrim_rows, width), BF),
@@ -398,7 +430,7 @@
         compiler_params=pltpu.CompilerParams(
             collective_id=0, has_side_effects=True, vmem_limit_bytes=56 * 1024 * 1024
         ),
-    )(embedded, norm_gain.astype(F32), shorts, medium_filters[0], out_weight[0])
+    )(embedded, norm_gain, short_filters, medium_filters, out_weight)
     return result[None]
 
 

time: 166 us -> 160 us (0.964)
  Pallas kernels: 159 us -> 155 us
    pallas_call x1, Pallas kernels: 159 us -> 155 us  [local(): pl.pallas_call(functools.partial(relay_kernel, sizes), out_shape=jax.Shap...]
where the time goes in v2:
time: 160 us
  Pallas kernels  155 us (97%)
  local copies, waits for them, and re-layouts  3.5 us (2%)
  matrix products  1.73 us (1%)
    pallas_call x1, Pallas kernels, local(): pl.pallas_call(functools.partial(relay_kernel, sizes), out_shape=jax.Shap...  155 us
    unnamed x4, local copies, waits for them, and re-layouts  3.5 us

profile of v2, /device:TPU:5, one launch (start us, length us, event | category | flops | bytes accessed | tf_op | source)
XLA Modules:
  0.0 159.8 jit_solution(3748999801636798768)
XLA Ops:
  0.0 0.0 copy-start
  0.0 0.8 copy.7
  0.8 0.5 copy-done
  1.2 1.7 %convolution_convert_fusion = bf16[512,1024]{1,0:T(8,128)(2,1)} fusion(bf16[512,1024]{1,0:T(8,128)(2,1)S(1)} %copy-done, s32[512]{0:T(512)S(1)} %bitcast.8), kind=kOutput, calls=%fused_computation | convolution fusion | flops 537657344 | bytes 2099200 | tf_op jit(solution)/shard_map/dot_general | solution.py:393
  3.0 154.6 %shard_map.64 = bf16[2,256,1024]{2,1,0:T(8,128)(2,1)} custom-call(bf16[2,256,1024]{2,1,0:T(8,128)(2,1)} %bitcast.6, bf16[1,1024]{1,0:T(2,128)(2,1)} %gain_ref.1, bf16[1,3,7,1024]{3,2,1,0:T(8,128)(2,1)} %short_ref.1, bf16[1,128,1024]{2,1,0:T(8,128)(2,1)} %med_ref.1, bf16[1,1024,1024]{2,1,0:T(8,128)(2,1)} %w_ref.1), custom_call_target="tpu_custom_call" | custom-call | tf_op jit(solution)/shard_map/pallas_call | solution.py:400
  157.5 2.3 %copy.9 = bf16[1,2,256,1024]{3,2,1,0:T(8,128)(2,1)} copy(bf16[1,2,256,1024]{3,2,1,0:T(8,128)(2,1)} %bitcast.5) | data formatting | bytes 2097152
Async XLA Ops:
  0.0 1.2 copy-start

commit v3 on v2

--- a/solution.py
+++ b/solution.py
@@ -60,17 +60,17 @@
 
     orders = (list(range(levels)), list(reversed(range(levels))))
 
-    def weight_copies(level, incoming=False):
+    def weight_copies(level, pieces, incoming=False):
         made = []
         for part in range(2):
             order = orders[part]
             flip = order[level]
             partner = seq + (1 - 2 * bit_of(flip)) * (1 << flip)
-            for k in range(1 << level):
+            for k in pieces:
                 shard = seq
                 theirs = partner
                 for i in range(level):
-                    change = (((k >> i) & 1) - bit_of(order[i])) * (1 << order[i])
+                    change = ((k >> i) & 1) * (1 - 2 * bit_of(order[i])) * (1 << order[i])
                     shard = shard + change
                     theirs = theirs + change
                 slot = (1 << level) - 1 + k
@@ -79,18 +79,20 @@
                 made.append(remote(place, place, w_send.at[part, slot], w_recv.at[part, slot], seq=partner))
         return made
 
-    def weights_start(level):
-        for out in weight_copies(level):
-            out.start()
+    def weights_start(stage):
+        pieces = range(1) if stage == 0 else range(1 << (stage - 1), 1 << stage)
+        for level in range(stage, levels):
+            for out in weight_copies(level, pieces):
+                out.start()
 
     def weights_arrive(level):
-        for into in weight_copies(level, True):
+        for into in weight_copies(level, range(1 << level), True):
             into.wait_recv()
 
     def weights_forward():
-        for level in range(1, levels):
-            weights_arrive(level - 1)
-            weights_start(level)
+        for stage in range(1, levels):
+            weights_arrive(stage - 1)
+            weights_start(stage)
 
     @pl.when(sec > 0)
     def _():
@@ -158,6 +160,28 @@
 
     row_chunk = 32
 
+    def own_squares(m, source):
+        def body(i, _):
+            part = pl.ds(pl.multiple_of(i * row_chunk, row_chunk), row_chunk)
+            value = source[m, part, :].astype(F32)
+            x[m, part, :] = value
+            summed = jnp.sum(value * value, axis=1, keepdims=True)
+            colb[part, :] = jnp.broadcast_to(summed, (row_chunk, LANES))
+            return 0
+
+        lax.fori_loop(0, rows // row_chunk, body, 0)
+        sqbuf[m, mp] = colb[...].T[0:8]
+
+    def send_squares(m):
+        for step in range(1, n_mp):
+            square_copy(m, step).start()
+
+    @pl.when(sec == 0)
+    def _():
+        for m in range(micro):
+            own_squares(m, emb_ref)
+            send_squares(m)
+
     def forward(m, step):
         for up in (True, False):
             here = (mp - step) if up else (mp + step)
@@ -170,6 +194,13 @@
                     if step < n_mp - 1:
                         gated_send(m, here, step, piece, up)
 
+    def weights_done():
+        weights_arrive(levels - 1)
+
+        @pl.when(sec < n_sec - 1)
+        def _():
+            pl.semaphore_signal(go_sem, inc=1, device_id={"section": sec + 1}, device_id_type=MESH)
+
     def front(m):
         pending = list(range(1, n_mp - 1)) if m > 0 else []
 
@@ -180,27 +211,9 @@
         @pl.when(sec > 0)
         def _():
             relay_in(m).wait_recv()
-
-        def squares(i, _):
-            part = pl.ds(pl.multiple_of(i * row_chunk, row_chunk), row_chunk)
-
-            @pl.when(sec == 0)
-            def _():
-                x[m, part, :] = emb_ref[m, part, :].astype(F32)
-
-            @pl.when(sec > 0)
-            def _():
-                x[m, part, :] = inbuf[m, part, :].astype(F32)
-
-            value = x[m, part, :]
-            summed = jnp.sum(value * value, axis=1, keepdims=True)
-            colb[part, :] = jnp.broadcast_to(summed, (row_chunk, LANES))
-            return 0
-
-        lax.fori_loop(0, rows // row_chunk, squares, 0)
-        sqbuf[m, mp] = colb[...].T[0:8]
-        for step in range(1, n_mp):
-            square_copy(m, step).start()
+            own_squares(m, inbuf)
+            send_squares(m)
+
         for step in range(1, n_mp):
             square_in(m, step).wait_recv()
         total = sqbuf[m, 0]
@@ -264,6 +277,10 @@
             @pl.when(sec == 0)
             def _():
                 weights_forward()
+        if m == min(1, micro - 1):
+            @pl.when(sec == 0)
+            def _():
+                weights_done()
 
         def filtering(block):
             taps_rows = 2 * rim
@@ -317,11 +334,9 @@
 
     def back(m):
         if m == 0:
-            weights_arrive(levels - 1)
-
-            @pl.when(sec < n_sec - 1)
+            @pl.when(sec > 0)
             def _():
-                pl.semaphore_signal(go_sem, inc=1, device_id={"section": sec + 1}, device_id_type=MESH)
+                weights_done()
 
         add_block(m, mp, True)
         for step in range(1, n_mp):
@@ -353,7 +368,7 @@
             back(m - 1)
 
     for level in range(levels):
-        for out in weight_copies(level):
+        for out in weight_copies(level, range(1 << level)):
             out.wait_send()
     for m in range(micro):
         @pl.when(sec < n_sec - 1)

time: 160 us -> 155 us (0.969)
  Pallas kernels: 155 us -> 149 us
    pallas_call x1, Pallas kernels: 155 us -> 149 us  [local(): pl.pallas_call(functools.partial(relay_kernel, sizes), out_shape=jax.Shap...]
where the time goes in v3:
time: 155 us
  Pallas kernels  149 us (96%)
  local copies, waits for them, and re-layouts  3.5 us (2%)
  matrix products  1.73 us (1%)
    pallas_call x1, Pallas kernels, local(): pl.pallas_call(functools.partial(relay_kernel, sizes), out_shape=jax.Shap...  149 us
    unnamed x4, local copies, waits for them, and re-layouts  3.5 us

profile of v3, /device:TPU:5, one launch (start us, length us, event | category | flops | bytes accessed | tf_op | source)
XLA Modules:
  0.0 154.6 jit_solution(7643895476641173738)
XLA Ops:
  0.0 0.0 copy-start
  0.0 0.8 copy.7
  0.8 0.5 copy-done
  1.2 1.7 %convolution_convert_fusion = bf16[512,1024]{1,0:T(8,128)(2,1)} fusion(bf16[512,1024]{1,0:T(8,128)(2,1)S(1)} %copy-done, s32[512]{0:T(512)S(1)} %bitcast.8), kind=kOutput, calls=%fused_computation | convolution fusion | flops 537657344 | bytes 2099200 | tf_op jit(solution)/shard_map/dot_general | solution.py:408
  3.0 149.4 %shard_map.64 = bf16[2,256,1024]{2,1,0:T(8,128)(2,1)} custom-call(bf16[2,256,1024]{2,1,0:T(8,128)(2,1)} %bitcast.6, bf16[1,1024]{1,0:T(2,128)(2,1)} %gain_ref.1, bf16[1,3,7,1024]{3,2,1,0:T(8,128)(2,1)} %short_ref.1, bf16[1,128,1024]{2,1,0:T(8,128)(2,1)} %med_ref.1, bf16[1,1024,1024]{2,1,0:T(8,128)(2,1)} %w_ref.1), custom_call_target="tpu_custom_call" | custom-call | tf_op jit(solution)/shard_map/pallas_call | solution.py:415
  152.4 2.3 %copy.9 = bf16[1,2,256,1024]{3,2,1,0:T(8,128)(2,1)} copy(bf16[1,2,256,1024]{3,2,1,0:T(8,128)(2,1)} %bitcast.5) | data formatting | bytes 2097152
Async XLA Ops:
  0.0 1.2 copy-start

commit v4 on v3

--- a/solution.py
+++ b/solution.py
@@ -80,9 +80,8 @@
         return made
 
     def weights_start(stage):
-        pieces = range(1) if stage == 0 else range(1 << (stage - 1), 1 << stage)
-        for level in range(stage, levels):
-            for out in weight_copies(level, pieces):
+        for level in (stage,):
+            for out in weight_copies(level, range(1 << stage)):
                 out.start()
 
     def weights_arrive(level):
@@ -197,11 +196,14 @@
     def weights_done():
         weights_arrive(levels - 1)
 
-        @pl.when(sec < n_sec - 1)
-        def _():
-            pl.semaphore_signal(go_sem, inc=1, device_id={"section": sec + 1}, device_id_type=MESH)
-
     def front(m):
+        if m == min(1, micro - 1):
+            @pl.when(sec < n_sec - 1)
+            def _():
+                pl.semaphore_signal(
+                    go_sem, inc=1, device_id={"section": sec + 1}, device_id_type=MESH
+                )
+
         pending = list(range(1, n_mp - 1)) if m > 0 else []
 
         def forward_one():

time: 155 us -> 146 us (0.942)
  Pallas kernels: 149 us -> 141 us
    pallas_call x1, Pallas kernels: 149 us -> 141 us  [local(): pl.pallas_call(functools.partial(relay_kernel, sizes), out_shape=jax.Shap...]
where the time goes in v4:
time: 146 us
  Pallas kernels  141 us (97%)
  local copies, waits for them, and re-layouts  3.5 us (2%)
  matrix products  1.73 us (1%)
    pallas_call x1, Pallas kernels, local(): pl.pallas_call(functools.partial(relay_kernel, sizes), out_shape=jax.Shap...  141 us
    unnamed x4, local copies, waits for them, and re-layouts  3.5 us

profile of v4, /device:TPU:5, one launch (start us, length us, event | category | flops | bytes accessed | tf_op | source)
XLA Modules:
  0.0 145.8 jit_solution(564385710990806240)
XLA Ops:
  0.0 0.0 copy-start
  0.0 0.8 copy.7
  0.8 0.5 copy-done
  1.2 1.7 %convolution_convert_fusion = bf16[512,1024]{1,0:T(8,128)(2,1)} fusion(bf16[512,1024]{1,0:T(8,128)(2,1)S(1)} %copy-done, s32[512]{0:T(512)S(1)} %bitcast.8), kind=kOutput, calls=%fused_computation | convolution fusion | flops 537657344 | bytes 2099200 | tf_op jit(solution)/shard_map/dot_general | solution.py:410
  3.0 140.6 %shard_map.64 = bf16[2,256,1024]{2,1,0:T(8,128)(2,1)} custom-call(bf16[2,256,1024]{2,1,0:T(8,128)(2,1)} %bitcast.6, bf16[1,1024]{1,0:T(2,128)(2,1)} %gain_ref.1, bf16[1,3,7,1024]{3,2,1,0:T(8,128)(2,1)} %short_ref.1, bf16[1,128,1024]{2,1,0:T(8,128)(2,1)} %med_ref.1, bf16[1,1024,1024]{2,1,0:T(8,128)(2,1)} %w_ref.1), custom_call_target="tpu_custom_call" | custom-call | tf_op jit(solution)/shard_map/pallas_call | solution.py:417
  143.5 2.3 %copy.9 = bf16[1,2,256,1024]{3,2,1,0:T(8,128)(2,1)} copy(bf16[1,2,256,1024]{3,2,1,0:T(8,128)(2,1)} %bitcast.5) | data formatting | bytes 2097152
Async XLA Ops:
  0.0 1.2 copy-start
